TPU v7x, 256 devices: a whole 4x4x8 slice. The times are simulated.
256 devices in a mesh: row: 16 (over x_hi, z), col: 8 (over x_lo, y), rep: 2 (over core).
Axes of the slice: x: 4 (x_hi: 2, x_lo: 2; x = x_hi * 2 + x_lo), y: 4, z: 8, core: 2. Of those that a mesh axis runs over, the one named last changes fastest.
Arguments:
- matrix: float32 [16384, 16384], P('row', 'col'), may hold values from -0.125 to 0.125
- vectors: float32 [64, 16384], P('rep', 'row'), may hold values from -0.3 to 0.3
Outputs:
- result: float32 [64, 16384], P('rep', 'row')
All inputs are finite; a program needn't handle non-finite values.
Results may differ from a plain program's by a relative error of at most 0.00011.
Values sent between devices are 32-bit elements; how exact they have to be, the bound alone decides.
A program may use at most 64 MiB of HBM per device.

v0:
```python
import jax
import jax.numpy as jnp
from jax import lax
from jax.sharding import PartitionSpec as P

TERMS = 6
STEPS = 1


def from_root(shard, axis, root):
    return lax.dynamic_index_in_dim(lax.all_gather(shard, axis), root, 0, keepdims=False)


def copy_for_each(shard, axis):
    count = lax.axis_size(axis)
    return lax.all_to_all(
        jnp.broadcast_to(shard[None], (count, *shard.shape)), axis, 0, 0, tiled=True
    )


def over_copies(shard, axis):
    return copy_for_each(shard, axis).sum(axis=0)


def apply_matrix(current, matrix):
    fanout = lax.axis_size("row") // lax.axis_size("col")
    column_index = lax.axis_index("col")
    pieces = [from_root(current, "row", column_index * fanout + which) for which in range(fanout)]
    operand = jnp.concatenate(pieces, axis=1)
    partial_value = lax.dot_general(
        operand,
        matrix,
        (((1,), (1,)), ((), ())),
        precision=lax.Precision.HIGHEST,
        preferred_element_type=jnp.float32,
    )
    return over_copies(partial_value, "col")


def local(matrix, vectors):
    summand = vectors
    running = vectors
    for degree in range(1, TERMS + 1):
        summand = apply_matrix(summand, matrix) / float(degree * STEPS)
        running = running + summand
    return running


def solution(mesh):
    placed = (P("row", "col"), P("rep", "row"))
    return jax.shard_map(
        local, mesh=mesh, in_specs=placed, out_specs=P("rep", "row"), check_vma=False
    )
```

profile of v0, /device:TPU:3, one launch (start us, length us, event | category | flops | bytes accessed | tf_op | source)
XLA Modules:
  0.0 671.6 jit_solution(11237662189762884529)
XLA Ops:
  7.3 86.4 %all-gather.13.cloned.1.call-done = f32[512,1024]{1,0:T(8,128)} async-done(((f32[32,1024]{1,0:T(8,128)}), f32[512,1024]{1,0:T(8,128)}) %all-gather.13.cloned.1.call-update) | async-done | bytes 2097168 | tf_op jit(solution)/shard_map/all_gather | solution.py:11
  93.7 1.0 dynamic-slice_bitcast_fusion.11
  94.7 10.0 %fusion = f32[32,1024]{1,0:T(8,128)S(1)} fusion(f32[1024,2048]{1,0:T(8,128)} %param.2, f32[32,1024]{1,0:T(8,128)S(1)} %get-tuple-element.16, f32[32,1024]{1,0:T(8,128)S(1)} %get-tuple-element.15), kind=kOutput, calls=%fused_computation | convolution fusion | flops 805371904 | bytes 8781824 | tf_op jit(solution)/shard_map/dot_general | solution.py:30
  104.8 14.5 %all_to_all.30 = f32[8,32,1024]{2,1,0:T(8,128)S(1)} all-to-all(f32[8,32,1024]{2,1,0:T(8,128)S(1)} %broadcast_in_dim.12), channel_id=1, replica_groups=mesh['row'=16,'col'=8,'rep'=2] {'col'}, dimensions={0} | all-to-all | bytes 2097152 | tf_op jit(solution)/shard_map/all_to_all | solution.py:16
  120.1 82.5 %all-gather.15.cloned.1.call-done = f32[512,1024]{1,0:T(8,128)} async-done(((f32[32,1024]{1,0:T(8,128)}), f32[512,1024]{1,0:T(8,128)}) %all-gather.15.cloned.1.call-update) | async-done | bytes 2097168 | tf_op jit(solution)/shard_map/all_gather | solution.py:11
  202.6 1.0 dynamic-slice_bitcast_fusion.9
  203.6 10.0 %fusion.4 = f32[32,1024]{1,0:T(8,128)S(1)} fusion(f32[1024,2048]{1,0:T(8,128)} %param.2, f32[32,1024]{1,0:T(8,128)S(1)} %get-tuple-element.14, f32[32,1024]{1,0:T(8,128)S(1)} %get-tuple-element.13), kind=kOutput, calls=%fused_computation.4 | convolution fusion | flops 805371904 | bytes 8781824 | tf_op jit(solution)/shard_map/dot_general | solution.py:30
  213.7 14.5 %all_to_all.31 = f32[8,32,1024]{2,1,0:T(8,128)S(1)} all-to-all(f32[8,32,1024]{2,1,0:T(8,128)S(1)} %broadcast_in_dim.13), channel_id=1, replica_groups=mesh['row'=16,'col'=8,'rep'=2] {'col'}, dimensions={0} | all-to-all | bytes 2097152 | tf_op jit(solution)/shard_map/all_to_all | solution.py:16
  229.0 82.5 %all-gather.17.cloned.1.call-done = f32[512,1024]{1,0:T(8,128)} async-done(((f32[32,1024]{1,0:T(8,128)}), f32[512,1024]{1,0:T(8,128)}) %all-gather.17.cloned.1.call-update) | async-done | bytes 2097168 | tf_op jit(solution)/shard_map/all_gather | solution.py:11
  311.5 1.0 dynamic-slice_bitcast_fusion.7
  312.5 10.0 %fusion.8 = f32[32,1024]{1,0:T(8,128)S(1)} fusion(f32[1024,2048]{1,0:T(8,128)} %param.2, f32[32,1024]{1,0:T(8,128)S(1)} %get-tuple-element.12, f32[32,1024]{1,0:T(8,128)S(1)} %get-tuple-element.11), kind=kOutput, calls=%fused_computation.8 | convolution fusion | flops 805371904 | bytes 8781824 | tf_op jit(solution)/shard_map/dot_general | solution.py:30
  322.6 14.5 %all_to_all.32 = f32[8,32,1024]{2,1,0:T(8,128)S(1)} all-to-all(f32[8,32,1024]{2,1,0:T(8,128)S(1)} %broadcast_in_dim.14), channel_id=1, replica_groups=mesh['row'=16,'col'=8,'rep'=2] {'col'}, dimensions={0} | all-to-all | bytes 2097152 | tf_op jit(solution)/shard_map/all_to_all | solution.py:16
  338.1 82.3 %all-gather.19.cloned.1.call-done = f32[512,1024]{1,0:T(8,128)} async-done(((f32[32,1024]{1,0:T(8,128)}), f32[512,1024]{1,0:T(8,128)}) %all-gather.19.cloned.1.call-update) | async-done | bytes 2097168 | tf_op jit(solution)/shard_map/all_gather | solution.py:11
  420.4 1.0 dynamic-slice_bitcast_fusion.5
  421.4 10.0 %fusion.12 = f32[32,1024]{1,0:T(8,128)S(1)} fusion(f32[1024,2048]{1,0:T(8,128)} %param.2, f32[32,1024]{1,0:T(8,128)S(1)} %get-tuple-element.10, f32[32,1024]{1,0:T(8,128)S(1)} %get-tuple-element.9), kind=kOutput, calls=%fused_computation.12 | convolution fusion | flops 805371904 | bytes 8781824 | tf_op jit(solution)/shard_map/dot_general | solution.py:30
  431.5 14.5 %all_to_all.33 = f32[8,32,1024]{2,1,0:T(8,128)S(1)} all-to-all(f32[8,32,1024]{2,1,0:T(8,128)S(1)} %broadcast_in_dim.15), channel_id=1, replica_groups=mesh['row'=16,'col'=8,'rep'=2] {'col'}, dimensions={0} | all-to-all | bytes 2097152 | tf_op jit(solution)/shard_map/all_to_all | solution.py:16
  446.8 82.5 %all-gather.21.cloned.1.call-done = f32[512,1024]{1,0:T(8,128)} async-done(((f32[32,1024]{1,0:T(8,128)}), f32[512,1024]{1,0:T(8,128)}) %all-gather.21.cloned.1.call-update) | async-done | bytes 2097168 | tf_op jit(solution)/shard_map/all_gather | solution.py:11
  529.3 1.0 dynamic-slice_bitcast_fusion.3
  530.3 10.0 %fusion.16 = f32[32,1024]{1,0:T(8,128)S(1)} fusion(f32[1024,2048]{1,0:T(8,128)} %param.2, f32[32,1024]{1,0:T(8,128)S(1)} %get-tuple-element.8, f32[32,1024]{1,0:T(8,128)S(1)} %get-tuple-element.7), kind=kOutput, calls=%fused_computation.16 | convolution fusion | flops 805371904 | bytes 8781824 | tf_op jit(solution)/shard_map/dot_general | solution.py:30
  540.4 14.6 %all_to_all.34 = f32[8,32,1024]{2,1,0:T(8,128)S(1)} all-to-all(f32[8,32,1024]{2,1,0:T(8,128)S(1)} %broadcast_in_dim.16), channel_id=1, replica_groups=mesh['row'=16,'col'=8,'rep'=2] {'col'}, dimensions={0} | all-to-all | bytes 2097152 | tf_op jit(solution)/shard_map/all_to_all | solution.py:16
  555.8 82.6 %all-gather.23.cloned.1.call-done = f32[512,1024]{1,0:T(8,128)} async-done(((f32[32,1024]{1,0:T(8,128)}), f32[512,1024]{1,0:T(8,128)}) %all-gather.23.cloned.1.call-update) | async-done | bytes 2097168 | tf_op jit(solution)/shard_map/all_gather | solution.py:11
  638.4 1.0 dynamic-slice_bitcast_fusion.1
  639.4 10.0 %fusion.20 = f32[32,1024]{1,0:T(8,128)S(1)} fusion(f32[1024,2048]{1,0:T(8,128)} %param.2, f32[32,1024]{1,0:T(8,128)S(1)} %get-tuple-element.6, f32[32,1024]{1,0:T(8,128)S(1)} %get-tuple-element.5), kind=kOutput, calls=%fused_computation.20 | convolution fusion | flops 805371904 | bytes 8781824 | tf_op jit(solution)/shard_map/dot_general | solution.py:30
  649.5 14.5 %all_to_all.35 = f32[8,32,1024]{2,1,0:T(8,128)S(1)} all-to-all(f32[8,32,1024]{2,1,0:T(8,128)S(1)} %broadcast_in_dim.17), channel_id=1, replica_groups=mesh['row'=16,'col'=8,'rep'=2] {'col'}, dimensions={0} | all-to-all | bytes 2097152 | tf_op jit(solution)/shard_map/all_to_all | solution.py:16
  (33 shorter events, 6.3 us)
Async XLA Ops:
  6.5 87.2 %all-gather.13.cloned.1.call-start = ((), (), s32[]{:S(2)}) async-start(), calls=%async_computation.6 | async-start | bytes 2228224 | tf_op jit(solution)/shard_map/all_gather | solution.py:11
  7.3 195.3 %all-gather.15.cloned.1.call-start = ((), (), s32[]{:S(2)}) async-start(), calls=%async_computation.7 | async-start | bytes 2228224 | tf_op jit(solution)/shard_map/all_gather | solution.py:11
  120.0 191.5 %all-gather.17.cloned.1.call-start = ((), (), s32[]{:S(2)}) async-start(), calls=%async_computation.8 | async-start | bytes 2228224 | tf_op jit(solution)/shard_map/all_gather | solution.py:11
  228.9 191.5 %all-gather.19.cloned.1.call-start = ((), (), s32[]{:S(2)}) async-start(), calls=%async_computation.9 | async-start | bytes 2228224 | tf_op jit(solution)/shard_map/all_gather | solution.py:11
  337.8 191.5 %all-gather.21.cloned.1.call-start = ((), (), s32[]{:S(2)}) async-start(), calls=%async_computation.10 | async-start | bytes 2228224 | tf_op jit(solution)/shard_map/all_gather | solution.py:11
  446.7 191.6 %all-gather.23.cloned.1.call-start = ((), (), s32[]{:S(2)}) async-start(), calls=%async_computation.11 | async-start | bytes 2228224 | tf_op jit(solution)/shard_map/all_gather | solution.py:11
  540.4 123.6 %copy-start = (f32[32,1024]{1,0:T(8,128)S(1)}, f32[32,1024]{1,0:T(8,128)}, u32[]{:S(2)}) copy-start(f32[32,1024]{1,0:T(8,128)} %reduce_sum.54) | copy-start | bytes 393220
  540.4 123.6 %copy-start.1 = (f32[32,1024]{1,0:T(8,128)S(1)}, f32[32,1024]{1,0:T(8,128)}, u32[]{:S(2)}) copy-start(f32[32,1024]{1,0:T(8,128)} %param.3) | copy-start | bytes 393220
Sparse Core Ops, SparseCore 0:
  9.9 83.7 all-gather.12
  120.2 82.3 all-gather.14
  229.1 82.4 all-gather.16
  338.0 82.3 all-gather.18
  446.9 82.3 all-gather.20
  555.9 82.3 all-gather.22
where the time goes:
time: 677 us; the launch traced here: 672 us
  waiting for transfers between devices  500 us (74%)
  blocking collectives  87.1 us (13%)
  matrix products  59.8 us (9%)
  between operations  13.6 us (2%)
    all_gather x6, waiting for transfers between devices, from_root(): lax.all_gather(shard, axis)  499 us
    all_to_all x6, blocking collectives, copy_for_each(): lax.all_to_all(jnp.broadcast_to(shard[None], (count, *shard.shape)), axis...  87.1 us
    dot_general x6, matrix products, apply_matrix(): lax.dot_general(operand, matrix, (((1,), (1,)), ((), ())), precision=lax....  59.8 us
  transfers between devices with their start and end apart: 6, of which 6 were waited for; matrix products, arithmetic and copies ran while one was open for 0% of the time, Pallas kernels for 0%

commit v1 on v0

v1 whole, which is shorter than its diff:
```python
import functools

import jax
import jax.numpy as jnp
from jax import lax
from jax.experimental import pallas as pl
from jax.experimental.pallas import tpu as pltpu
from jax.sharding import PartitionSpec as P

TERMS = 6
STEPS = 1
MESH = pl.DeviceIdType.MESH
BF16 = jnp.bfloat16
F32 = jnp.float32
LANES = 128
ORDER = (4, 3, 5, 2, 6, 1, 7, 0)


def halves(value):
    high = value.astype(BF16)
    return high, (value - high.astype(F32)).astype(BF16)


def kernel(
    rows, cols, mat_ref, vec_ref, out_ref,
    stage, a_high, a_low, operand, xin, part, arrived, total, final, running,
    load_sem, x_send, x_recv, p_send, p_recv, f_send, f_recv,
):
    r, c = lax.axis_index("row"), lax.axis_index("col")
    blocks = rows // cols
    pieces = blocks * cols
    height = vec_ref.shape[0]
    home = lax.div(r, blocks)
    slot = lax.rem(r, blocks) * cols + c
    mine = home == c
    half, ring = rows // 8, 8
    chunks = stage.shape[0]
    depth = stage.shape[1]

    loads = [
        pltpu.make_async_copy(mat_ref.at[pl.ds(n * depth, depth), :], stage.at[n], load_sem.at[n])
        for n in range(chunks)
    ]
    for load in loads:
        load.start()

    barrier = pltpu.get_barrier_semaphore()
    for step in range(1, cols):
        pl.semaphore_signal(
            barrier, inc=1, device_id={"col": lax.rem(c + step, cols)}, device_id_type=MESH
        )
    for block in range(blocks):
        for k in range(cols):
            source = c * blocks + block
            itself = jnp.logical_and(source == r, c == k)

            @pl.when(jnp.logical_not(itself))
            def _():
                pl.semaphore_signal(
                    barrier, inc=1, device_id={"row": source, "col": k}, device_id_type=MESH
                )

    total[0] = vec_ref[:, pl.ds(pl.multiple_of(c * LANES, LANES), LANES)]
    running[...] = total[0]

    @pl.when(mine)
    def _():
        pl.semaphore_wait(barrier, cols - 1 + rows - 1)

    @pl.when(jnp.logical_not(mine))
    def _():
        pl.semaphore_wait(barrier, cols - 1 + rows)

    z, hi = lax.rem(r, ring), lax.div(r, ring)

    def spread(degree):
        for step in ORDER:
            for side in range(half):
                target = lax.rem(hi + 1 + side, half) * ring + lax.rem(z + step, ring)
                copy = pltpu.make_async_remote_copy(
                    src_ref=total.at[degree],
                    dst_ref=xin.at[degree, slot],
                    send_sem=x_send.at[degree],
                    recv_sem=x_recv.at[degree, slot],
                    device_id={"row": target, "col": home},
                    device_id_type=MESH,
                )
                if step == 0 and side == half - 1:
                    pl.when(jnp.logical_not(mine))(copy.start)

                    @pl.when(mine)
                    def _():
                        xin[degree, slot] = total[degree]
                else:
                    copy.start()

    def sent(degree):
        count = pl.ds(0, rows - 1)

        @pl.when(mine)
        def _():
            pltpu.make_async_copy(
                xin.at[degree, count], xin.at[degree, count], x_send.at[degree]
            ).wait()

        @pl.when(jnp.logical_not(mine))
        def _():
            pltpu.make_async_copy(xin.at[degree], xin.at[degree], x_send.at[degree]).wait()

    spread(0)

    for n in range(chunks):
        loads[n].wait()
        high, low = halves(stage[n])
        a_high[n * depth : (n + 1) * depth] = high
        a_low[n * depth : (n + 1) * depth] = low

    wide = 2 * LANES

    def one_degree(degree, carry):
        for p in range(pieces):
            itself = jnp.logical_and(mine, slot == p)

            @pl.when(jnp.logical_not(itself))
            def _():
                pltpu.make_async_copy(
                    xin.at[degree, p], xin.at[degree, p], x_recv.at[degree, p]
                ).wait()

            high, low = halves(xin[degree, p])
            operand[0:height, p * LANES : (p + 1) * LANES] = high
            operand[height : 2 * height, p * LANES : (p + 1) * LANES] = low
        for step in range(1, cols // 2 + 1):
            pair = lax.rem(lax.div(c, 2) + step, cols // 2)
            window = pl.ds(pl.multiple_of(pair * wide, wide), wide)
            value = lax.dot_general(
                operand[...], a_high[window, :], (((1,), (1,)), ((), ())), preferred_element_type=F32
            )
            value += lax.dot_general(
                operand[...], a_low[window, :], (((1,), (1,)), ((), ())), preferred_element_type=F32
            )
            value = value[:height] + value[height:]
            for which in range(2):
                k = pair * 2 + which
                piece = value[:, which * LANES : (which + 1) * LANES]
                if step < cols // 2:
                    part[degree, k] = piece
                    pltpu.make_async_remote_copy(
                        src_ref=part.at[degree, k],
                        dst_ref=arrived.at[degree, c],
                        send_sem=p_send.at[degree],
                        recv_sem=p_recv.at[degree],
                        device_id={"col": k},
                        device_id_type=MESH,
                    ).start()
                else:
                    part[degree, k] = piece

                    @pl.when(k != c)
                    def _():
                        pltpu.make_async_remote_copy(
                            src_ref=part.at[degree, k],
                            dst_ref=arrived.at[degree, c],
                            send_sem=p_send.at[degree],
                            recv_sem=p_recv.at[degree],
                            device_id={"col": k},
                            device_id_type=MESH,
                        ).start()

        others = pl.ds(0, cols - 1)
        pltpu.make_async_copy(
            arrived.at[degree, others], arrived.at[degree, others], p_recv.at[degree]
        ).wait()
        arrived[degree, c] = part[degree, c]
        summed = arrived[degree, 0]
        for k in range(1, cols):
            summed = summed + arrived[degree, k]
        summed = summed / ((degree + 1) * STEPS).astype(F32)
        running[...] += summed

        @pl.when(degree < TERMS - 1)
        def _():
            total[degree + 1] = summed
            spread(degree + 1)

        sent(degree)
        pltpu.make_async_copy(
            arrived.at[degree, others], arrived.at[degree, others], p_send.at[degree]
        ).wait()
        return carry

    lax.fori_loop(0, TERMS, one_degree, 0)

    for step in range(1, cols):
        pltpu.make_async_remote_copy(
            src_ref=running,
            dst_ref=final.at[c],
            send_sem=f_send,
            recv_sem=f_recv,
            device_id={"col": lax.rem(c + step, cols)},
            device_id_type=MESH,
        ).start()
    others = pl.ds(0, cols - 1)
    pltpu.make_async_copy(final.at[others], final.at[others], f_recv).wait()
    final[c] = running[...]
    for k in range(cols):
        out_ref[:, k * LANES : (k + 1) * LANES] = final[k]
    pltpu.make_async_copy(final.at[others], final.at[others], f_send).wait()


def local(rows, cols, matrix, vectors):
    height, width = vectors.shape
    tall, deep = matrix.shape
    pieces = rows // cols * cols
    chunks = 8
    return pl.pallas_call(
        functools.partial(kernel, rows, cols),
        out_shape=jax.ShapeDtypeStruct(vectors.shape, F32),
        in_specs=[
            pl.BlockSpec(memory_space=pl.ANY),
            pl.BlockSpec(memory_space=pltpu.VMEM),
        ],
        out_specs=pl.BlockSpec(memory_space=pltpu.VMEM),
        scratch_shapes=[
            pltpu.VMEM((chunks, tall // chunks, deep), F32),
            pltpu.VMEM((tall, deep), BF16),
            pltpu.VMEM((tall, deep), BF16),
            pltpu.VMEM((2 * height, deep), BF16),
            pltpu.VMEM((TERMS, pieces, height, LANES), F32),
            pltpu.VMEM((TERMS, cols, height, LANES), F32),
            pltpu.VMEM((TERMS, cols, height, LANES), F32),
            pltpu.VMEM((TERMS, height, LANES), F32),
            pltpu.VMEM((cols, height, LANES), F32),
            pltpu.VMEM((height, LANES), F32),
            pltpu.SemaphoreType.DMA((chunks,)),
            pltpu.SemaphoreType.DMA((TERMS,)),
            pltpu.SemaphoreType.DMA((TERMS, pieces)),
            pltpu.SemaphoreType.DMA((TERMS,)),
            pltpu.SemaphoreType.DMA((TERMS,)),
            pltpu.SemaphoreType.DMA,
            pltpu.SemaphoreType.DMA,
        ],
        compiler_params=pltpu.CompilerParams(
            collective_id=0, has_side_effects=True, vmem_limit_bytes=60 * 2**20
        ),
    )(matrix, vectors)


def solution(mesh):
    rows, cols = mesh.shape["row"], mesh.shape["col"]
    return jax.shard_map(
        functools.partial(local, rows, cols),
        mesh=mesh,
        in_specs=(P("row", "col"), P("rep", "row")),
        out_specs=P("rep", "row"),
        check_vma=False,
    )
```

time: 677 us -> 116 us (0.17)
  the two profiles are of different devices: /device:TPU:3 before, /device:TPU:2 now
where the time goes in v1:
time: 116 us
  Pallas kernels  115 us (99%)
  local copies, waits for them, and re-layouts  1.57 us (1%)
    pallas_call x1, Pallas kernels, local(): pl.pallas_call(functools.partial(kernel, rows, cols), out_shape=jax.Shape...  115 us

profile of v1, /device:TPU:2, one launch (start us, length us, event | category | flops | bytes accessed | tf_op | source)
XLA Modules:
  0.0 116.3 jit_solution(915559351378153322)
XLA Ops:
  0.0 114.7 %shard_map.28 = f32[32,1024]{1,0:T(8,128)} custom-call(f32[1024,2048]{1,0:T(8,128)} %mat_ref.1, f32[32,1024]{1,0:T(8,128)} %vec_ref.1), custom_call_target="tpu_custom_call" | custom-call | tf_op jit(solution)/shard_map/pallas_call | solution.py:216
  114.7 1.6 %copy.4 = f32[32,1024]{1,0:T(8,128)} copy(f32[32,1024]{1,0:T(8,128)} %shard_map.28) | data formatting | bytes 262144
